TPU v7x, 128 devices: a whole 4x4x4 slice. The times are simulated.
128 devices in a mesh: local: 2 (over core), data: 64 (over z, y, x).
Axes of the slice: x: 4, y: 4, z: 4, core: 2. Of those that a mesh axis runs over, the one named last changes fastest.
Arguments:
- tokens: bfloat16 [65536, 1024], P(('data', 'local'))
- cotangent: bfloat16 [65536, 1024], P(('data', 'local'))
- w_up: bfloat16 [4, 1024, 4096], P(None, ('data', 'local'))
- w_down: bfloat16 [4, 4096, 1024], P(None, ('data', 'local'))
- lora_a: float32 [4, 1024, 8], replicated
- lora_b: float32 [4, 8, 4096], replicated
Outputs:
- output 1: bfloat16 [65536, 1024], P(('data', 'local'))
- output 2: bfloat16 [65536, 1024], P(('data', 'local'))
- output 3: float32 [4, 1024, 8], replicated
- output 4: float32 [4, 8, 4096], replicated
All inputs are finite; a program needn't handle non-finite values.
Results may differ from a plain program's by a relative error of at most 0.0188455.
Values are sent between devices in bfloat16 or wider.
A program may use at most 1 GiB of HBM per device.

v0:
```python
import jax
import jax.numpy as jnp
from jax import lax
from jax.sharding import PartitionSpec as P

GROUP = ("data", "local")
NORM_EPS = 1e-6
FULL_PRECISION = lax.Precision.HIGHEST


def gelu_tanh(pre_f):
    return jax.nn.gelu(pre_f, approximate=True)


def layer_forward(resid, full_up, full_down, adapt_a, adapt_b):
    resid_f = resid.astype(jnp.float32)
    inv_rms = lax.rsqrt(jnp.mean(resid_f * resid_f, axis=-1, keepdims=True) + NORM_EPS)
    normed = (resid_f * inv_rms).astype(jnp.bfloat16)
    low_rank = jnp.dot(normed, adapt_a, precision=FULL_PRECISION, preferred_element_type=jnp.float32)
    pre_act = (jnp.dot(normed, full_up, preferred_element_type=jnp.float32) + jnp.dot(low_rank, adapt_b, precision=FULL_PRECISION, preferred_element_type=jnp.float32)).astype(jnp.bfloat16)
    hidden_act = gelu_tanh(pre_act.astype(jnp.float32)).astype(jnp.bfloat16)
    new_resid = (resid_f + jnp.dot(hidden_act, full_down, preferred_element_type=jnp.float32)).astype(jnp.bfloat16)
    return new_resid, (resid, inv_rms, normed, low_rank, pre_act)


def layer_backward(d_resid, saved, full_up, full_down, adapt_a, adapt_b):
    resid, inv_rms, normed, low_rank, pre_act = saved
    d_hidden = jnp.einsum("th,fh->tf", d_resid, full_down, preferred_element_type=jnp.float32).astype(jnp.bfloat16)
    gelu_pull = jax.vjp(gelu_tanh, pre_act.astype(jnp.float32))[1]
    d_pre = gelu_pull(d_hidden.astype(jnp.float32))[0].astype(jnp.bfloat16)
    d_low = jnp.einsum("tf,rf->tr", d_pre, adapt_b, precision=FULL_PRECISION, preferred_element_type=jnp.float32)
    grad_b = jnp.einsum("tr,tf->rf", low_rank, d_pre, precision=FULL_PRECISION, preferred_element_type=jnp.float32)
    grad_a = jnp.einsum("th,tr->hr", normed, d_low, precision=FULL_PRECISION, preferred_element_type=jnp.float32)
    d_main = jnp.einsum("tf,hf->th", d_pre, full_up, preferred_element_type=jnp.float32).astype(jnp.bfloat16)
    d_side = jnp.einsum("tr,hr->th", d_low, adapt_a, precision=FULL_PRECISION, preferred_element_type=jnp.float32).astype(jnp.bfloat16)
    d_norm_f = (d_main + d_side).astype(jnp.float32)
    resid_f = resid.astype(jnp.float32)
    row_dot = jnp.mean(resid_f * d_norm_f, axis=-1, keepdims=True)
    d_resid_f = d_resid.astype(jnp.float32) + inv_rms * d_norm_f - resid_f * (inv_rms * inv_rms * inv_rms) * row_dot
    return d_resid_f.astype(jnp.bfloat16), grad_a, grad_b


def solution(mesh):
    data_size = mesh.shape["data"]
    tok_spec = P(GROUP, None)
    weight_spec = P(None, GROUP, None)

    def device_step(tokens, cotangent, up_shards, down_shards, value_a6, array_b6):
        local_idx = lax.axis_index("local")
        num_layers = up_shards.shape[0]
        up_rows = up_shards.shape[1] * data_size
        down_rows = down_shards.shape[1] * data_size
        resid = tokens
        kept = []
        for layer in range(num_layers):
            full_up = lax.all_gather(up_shards[layer], GROUP, axis=0, tiled=True)
            full_down = lax.all_gather(down_shards[layer], GROUP, axis=0, tiled=True)
            resid, saved = layer_forward(resid, full_up, full_down, value_a6[layer], array_b6[layer])
            keep_up = lax.dynamic_slice_in_dim(full_up, local_idx * up_rows, up_rows, axis=0)
            keep_down = lax.dynamic_slice_in_dim(full_down, local_idx * down_rows, down_rows, axis=0)
            kept.append((saved, keep_up, keep_down))
        d_resid = cotangent
        grads_a = []
        grads_b = []
        for layer in reversed(range(num_layers)):
            saved, keep_up, keep_down = kept[layer]
            full_up = lax.all_gather(keep_up, "local", axis=0, tiled=True)
            full_down = lax.all_gather(keep_down, "local", axis=0, tiled=True)
            d_resid, grad_a, grad_b = layer_backward(d_resid, saved, full_up, full_down, value_a6[layer], array_b6[layer])
            grad_a, grad_b = lax.psum((grad_a, grad_b), GROUP)
            grads_a.insert(0, grad_a)
            grads_b.insert(0, grad_b)
        return resid, d_resid, jnp.stack(grads_a), jnp.stack(grads_b)

    return jax.shard_map(device_step, mesh=mesh, in_specs=(tok_spec, tok_spec, weight_spec, weight_spec, P(), P()), out_specs=(tok_spec, tok_spec, P(), P()), check_vma=False)
```

profile of v0, /device:TPU:1, one launch (start us, length us, event | category | flops | bytes accessed | tf_op | source)
XLA Modules:
  0.0 1116.3 jit_solution(3117936182070583427)
XLA Ops:
  14.6 70.1 %all-gather.47.cloned.1.call-done = bf16[1,4096,1024]{2,1,0:T(8,128)(2,1)} async-done(((bf16[1,32,1024]{2,1,0:T(8,128)(2,1)}), bf16[1,4096,1024]{2,1,0:T(8,128)(2,1)}) %all-gather.47.cloned.1.call-update) | async-done | bytes 8388624 | tf_op jit(solution)/shard_map/all_gather | solution.py:57
  89.5 65.4 %all-gather.45.cloned.1.call-done = bf16[1,1024,4096]{2,1,0:T(8,128)(2,1)} async-done(((bf16[1,8,4096]{2,1,0:T(8,128)(2,1)}), bf16[1,1024,4096]{2,1,0:T(8,128)(2,1)}) %all-gather.45.cloned.1.call-update) | async-done | bytes 8388624 | tf_op jit(solution)/shard_map/all_gather | solution.py:56
  159.7 66.0 %all-gather.43.cloned.1.call-done = bf16[1,4096,1024]{2,1,0:T(8,128)(2,1)} async-done(((bf16[1,32,1024]{2,1,0:T(8,128)(2,1)}), bf16[1,4096,1024]{2,1,0:T(8,128)(2,1)}) %all-gather.43.cloned.1.call-update) | async-done | bytes 8388624 | tf_op jit(solution)/shard_map/all_gather | solution.py:57
  230.4 65.3 %all-gather.41.cloned.1.call-done = bf16[1,1024,4096]{2,1,0:T(8,128)(2,1)} async-done(((bf16[1,8,4096]{2,1,0:T(8,128)(2,1)}), bf16[1,1024,4096]{2,1,0:T(8,128)(2,1)}) %all-gather.41.cloned.1.call-update) | async-done | bytes 8388624 | tf_op jit(solution)/shard_map/all_gather | solution.py:56
  300.5 65.8 %all-gather.39.cloned.1.call-done = bf16[1,4096,1024]{2,1,0:T(8,128)(2,1)} async-done(((bf16[1,32,1024]{2,1,0:T(8,128)(2,1)}), bf16[1,4096,1024]{2,1,0:T(8,128)(2,1)}) %all-gather.39.cloned.1.call-update) | async-done | bytes 8388624 | tf_op jit(solution)/shard_map/all_gather | solution.py:57
  370.9 65.4 %all-gather.37.cloned.1.call-done = bf16[1,1024,4096]{2,1,0:T(8,128)(2,1)} async-done(((bf16[1,8,4096]{2,1,0:T(8,128)(2,1)}), bf16[1,1024,4096]{2,1,0:T(8,128)(2,1)}) %all-gather.37.cloned.1.call-update) | async-done | bytes 8388624 | tf_op jit(solution)/shard_map/all_gather | solution.py:56
  443.1 63.4 %all-gather.33.cloned.1.call-done = bf16[1,1024,4096]{2,1,0:T(8,128)(2,1)} async-done(((bf16[1,8,4096]{2,1,0:T(8,128)(2,1)}), bf16[1,1024,4096]{2,1,0:T(8,128)(2,1)}) %all-gather.33.cloned.1.call-update) | async-done | bytes 8388624 | tf_op jit(solution)/shard_map/all_gather | solution.py:56
  513.6 8.9 add_convert_fusion.3
  522.5 54.7 %all-gather.35.cloned.1.call-done = bf16[1,4096,1024]{2,1,0:T(8,128)(2,1)} async-done(((bf16[1,32,1024]{2,1,0:T(8,128)(2,1)}), bf16[1,4096,1024]{2,1,0:T(8,128)(2,1)}) %all-gather.35.cloned.1.call-update) | async-done | bytes 8388624 | tf_op jit(solution)/shard_map/all_gather | solution.py:57
  577.3 10.3 fusion.125
  607.3 10.5 fusion.130
  640.5 10.3 fusion.62
  650.8 8.3 fusion.85
  659.2 15.0 %fusion.15 = (bf16[512,4096]{1,0:T(8,128)(2,1)S(1)}, bf16[512,4096]{1,0:T(8,128)(2,1)}) fusion(bf16[4096,512]{0,1:T(8,128)(2,1)S(1)} %fusion.85, f32[512,4096]{1,0:T(8,128)S(1)} %copy-done.31, f32[512,8]{0,1:T(8,128)S(1)} %fusion.199, f32[4,8,4096]{2,1,0:T(8,128)S(1)} %copy-done.16), kind=kOutput, calls=%fused_computation.38 | convolution fusion | flops 251658240 | bytes 21118976 | tf_op jit(solution)/shard_map/dot_general | solution.py:20
  679.5 9.3 fusion.144
  691.7 12.3 %fusion.6 = bf16[512,4096]{1,0:T(8,128)(2,1)S(1)} fusion(bf16[512,4096]{1,0:T(8,128)(2,1)} %copy-done.12, bf16[512,1024]{1,0:T(8,128)(2,1)S(1)} %fusion.110, bf16[1,4096,1024]{2,1,0:T(8,128)(2,1)} %all-gather.53.cloned.1.call-done), kind=kOutput, calls=%fused_computation.29 | convolution fusion | flops 4343201792 | bytes 17825792 | tf_op jit(solution)/shard_map/th,fh->tf/dot_general | solution.py:28
  710.2 9.2 fusion.147
  723.2 12.7 %fusion.9 = bf16[512,4096]{1,0:T(8,128)(2,1)S(1)} fusion(bf16[512,4096]{1,0:T(8,128)(2,1)} %copy-done.11, bf16[512,1024]{1,0:T(8,128)(2,1)} %fusion.113, bf16[1,4096,1024]{2,1,0:T(8,128)(2,1)} %all-gather.57.cloned.1.call-done), kind=kOutput, calls=%fused_computation.32 | convolution fusion | flops 4343201792 | bytes 17825792 | tf_op jit(solution)/shard_map/th,fh->tf/dot_general | solution.py:28
  744.4 9.2 fusion.150
  758.8 12.2 %fusion.12 = bf16[512,4096]{1,0:T(8,128)(2,1)S(1)} fusion(bf16[512,4096]{1,0:T(8,128)(2,1)} %add_convert_fusion.3, bf16[512,1024]{1,0:T(8,128)(2,1)S(1)} %fusion.116, bf16[1,4096,1024]{2,1,0:T(8,128)(2,1)} %all-gather.61.cloned.1.call-done), kind=kOutput, calls=%fused_computation.35 | convolution fusion | flops 4343201792 | bytes 17825792 | tf_op jit(solution)/shard_map/th,fh->tf/dot_general | solution.py:28
  792.8 9.5 fusion.153
  806.0 11.1 fusion.137
  818.7 134.7 %all-reduce.5.cloned.1.call-done = (f32[1,1024,8]{1,2,0:T(8,128)}, f32[1,1024,8]{1,2,0:T(8,128)}, f32[1,1024,8]{1,2,0:T(8,128)}, f32[1,1024,8]{1,2,0:T(8,128)}) async-done(((f32[1,1024,8]{1,2,0:T(8,128)}, f32[1,1024,8]{1,2,0:T(8,128)}, f32[1,1024,8]{1,2,0:T(8,128)}, f32[1,1024,8]{1,2,0:T(8,128)}), (f32[1,1024,8]{1,2,0:T(8,128)}, f32[1,1024,8]{1,2,0:T(8,128)}, f32[1,1024,8]{1,2,0:T(8,128)}, ...) | async-done | bytes 131088 | tf_op jit(solution)/shard_map/psum | solution.py:70
  954.9 152.4 %all-reduce.7.cloned.1.call-done = (f32[1,8,4096]{2,1,0:T(8,128)}, f32[1,8,4096]{2,1,0:T(8,128)}, f32[1,8,4096]{2,1,0:T(8,128)}, f32[1,8,4096]{2,1,0:T(8,128)}) async-done(((f32[1,8,4096]{2,1,0:T(8,128)}, f32[1,8,4096]{2,1,0:T(8,128)}, f32[1,8,4096]{2,1,0:T(8,128)}, f32[1,8,4096]{2,1,0:T(8,128)}), (f32[1,8,4096]{2,1,0:T(8,128)}, f32[1,8,4096]{2,1,0:T(8,128)}, f32[1,8,4096]{2,1,0:T(8,128)}, ...) | async-done | bytes 524304 | tf_op jit(solution)/shard_map/psum | solution.py:70
  (174 shorter events, 149.3 us)
Async XLA Ops:
  7.2 77.5 %all-gather.47.cloned.1.call-start = ((), (), s32[]{:S(2)}) async-start(), calls=%async_computation.7 | async-start | bytes 8454144 | tf_op jit(solution)/shard_map/all_gather | solution.py:57
  8.9 146.0 %all-gather.45.cloned.1.call-start = ((), (), s32[]{:S(2)}) async-start(), calls=%async_computation.6 | async-start | bytes 8454144 | tf_op jit(solution)/shard_map/all_gather | solution.py:56
  10.6 215.1 %all-gather.43.cloned.1.call-start = ((), (), s32[]{:S(2)}) async-start(), calls=%async_computation.5 | async-start | bytes 8454144 | tf_op jit(solution)/shard_map/all_gather | solution.py:57
  11.3 284.4 %all-gather.41.cloned.1.call-start = ((), (), s32[]{:S(2)}) async-start(), calls=%async_computation.4 | async-start | bytes 8454144 | tf_op jit(solution)/shard_map/all_gather | solution.py:56
  11.9 354.4 %all-gather.39.cloned.1.call-start = ((), (), s32[]{:S(2)}) async-start(), calls=%async_computation.3 | async-start | bytes 8454144 | tf_op jit(solution)/shard_map/all_gather | solution.py:57
  12.5 423.8 %all-gather.37.cloned.1.call-start = ((), (), s32[]{:S(2)}) async-start(), calls=%async_computation.2 | async-start | bytes 8454144 | tf_op jit(solution)/shard_map/all_gather | solution.py:56
  13.1 493.5 %all-gather.33.cloned.1.call-start = ((), (), s32[]{:S(2)}) async-start(), calls=%async_computation | async-start | bytes 8454144 | tf_op jit(solution)/shard_map/all_gather | solution.py:56
  13.8 563.5 %all-gather.35.cloned.1.call-start = ((), (), s32[]{:S(2)}) async-start(), calls=%async_computation.1 | async-start | bytes 8454144 | tf_op jit(solution)/shard_map/all_gather | solution.py:57
  14.6 636.3 %all-gather.49.cloned.1.call-start = ((), (), s32[]{:S(2)}) async-start(), calls=%async_computation.8 | async-start | bytes 12582912 | tf_op jit(solution)/shard_map/all_gather | solution.py:68
  89.5 590.0 %all-gather.51.cloned.1.call-start = ((), (), s32[]{:S(2)}) async-start(), calls=%async_computation.9 | async-start | bytes 12582912 | tf_op jit(solution)/shard_map/all_gather | solution.py:67
  159.6 532.1 %all-gather.53.cloned.1.call-start = ((), (), s32[]{:S(2)}) async-start(), calls=%async_computation.10 | async-start | bytes 12582912 | tf_op jit(solution)/shard_map/all_gather | solution.py:68
  230.3 479.8 %all-gather.55.cloned.1.call-start = ((), (), s32[]{:S(2)}) async-start(), calls=%async_computation.11 | async-start | bytes 12582912 | tf_op jit(solution)/shard_map/all_gather | solution.py:67
  300.4 422.8 %all-gather.57.cloned.1.call-start = ((), (), s32[]{:S(2)}) async-start(), calls=%async_computation.12 | async-start | bytes 12582912 | tf_op jit(solution)/shard_map/all_gather | solution.py:68
  370.9 70.4 %copy-start = (bf16[512,1024]{1,0:T(8,128)(2,1)S(1)}, bf16[512,1024]{1,0:T(8,128)(2,1)}, u32[]{:S(2)}) copy-start(bf16[512,1024]{1,0:T(8,128)(2,1)} %param.6) | copy-start | bytes 3145732
  370.9 71.3 %copy-start.18 = (f32[4,1024,8]{1,2,0:T(8,128)S(1)}, f32[4,1024,8]{1,2,0:T(8,128)}, u32[]{:S(2)}) copy-start(f32[4,1024,8]{1,2,0:T(8,128)} %param.10) | copy-start | bytes 393220
  370.9 373.5 %all-gather.59.cloned.1.call-start = ((), (), s32[]{:S(2)}) async-start(), calls=%async_computation.13 | async-start | bytes 12582912 | tf_op jit(solution)/shard_map/all_gather | solution.py:67
  441.0 317.7 %all-gather.61.cloned.1.call-start = ((), (), s32[]{:S(2)}) async-start(), calls=%async_computation.14 | async-start | bytes 12582912 | tf_op jit(solution)/shard_map/all_gather | solution.py:68
  442.1 71.5 %copy-start.25 = (f32[512]{0:T(512)}, f32[512]{0:T(512)S(1)}, u32[]{:S(2)}) copy-start(f32[512]{0:T(512)S(1)} %get-tuple-element.21) | copy-start | bytes 6148
  443.1 70.5 %copy-start.19 = (f32[512,8]{0,1:T(8,128)}, f32[512,8]{0,1:T(8,128)S(1)}, u32[]{:S(2)}) copy-start(f32[512,8]{0,1:T(8,128)S(1)} %fusion.208) | copy-start | bytes 49156
  443.1 70.5 %copy-start.15 = (f32[4,8,4096]{2,1,0:T(8,128)S(1)}, f32[4,8,4096]{2,1,0:T(8,128)}, u32[]{:S(2)}) copy-start(f32[4,8,4096]{2,1,0:T(8,128)} %param.11) | copy-start | bytes 1572868
  590.6 202.1 %all-gather.63.cloned.1.call-start = ((), (), s32[]{:S(2)}) async-start(), calls=%async_computation.15 | async-start | bytes 12582912 | tf_op jit(solution)/shard_map/all_gather | solution.py:67
  599.7 31.4 %slice-start = ((s8[8388608]{0:T(1024)(128)(4,1)}), s8[4194304]{0:T(1024)(128)(4,1)S(1)}, s32[]{:S(2)}) async-start(s8[8388608]{0:T(1024)(128)(4,1)} %bitcast.191), calls=%async_computation.18 | async-start | bytes 8388608
  640.5 313.0 %all-reduce.5.cloned.1.call-start = ((), (), s32[]{:S(2)}) async-start(), calls=%async_computation.16 | async-start | bytes 262144 | tf_op jit(solution)/shard_map/psum | solution.py:70
  805.3 302.0 %all-reduce.7.cloned.1.call-start = ((), (), s32[]{:S(2)}) async-start(), calls=%async_computation.17 | async-start | bytes 1048576 | tf_op jit(solution)/shard_map/psum | solution.py:70
  (32 other events, 360.9 us)
Sparse Core Ops, SparseCore 0:
  11.5 73.1 all-gather.46
  87.7 67.1 all-gather.44
  158.5 67.1 all-gather.42
  228.5 67.1 all-gather.40
  299.1 67.1 all-gather.38
  369.1 67.1 all-gather.36
  439.3 67.1 all-gather.32
  510.1 67.1 all-gather.34
  578.9 21.1 all-gather.48
  601.6 24.8 all-gather.50
  628.2 24.8 all-gather.52
  654.6 24.8 all-gather.54
  681.1 24.8 all-gather.56
  707.5 24.8 all-gather.58
  733.9 24.8 all-gather.60
  760.3 24.8 all-gather.62
  805.5 147.9 all-reduce.4
  959.2 148.0 all-reduce.6
where the time goes:
time: 1120 us
  waiting for transfers between devices  810 us (72%)
  matrix products  237 us (21%)
  local copies, waits for them, and re-layouts  43.2 us (4%)
  between operations  15 us (1%)
    psum x2, waiting for transfers between devices, device_step(): grad_a, grad_b = lax.psum((grad_a, grad_b), GROUP)  287 us
    all_gather x4, waiting for transfers between devices, device_step(): full_up = lax.all_gather(up_shards[layer], GROUP, axis=0, tiled=True)  259 us
    all_gather x4, waiting for transfers between devices, device_step(): full_down = lax.all_gather(down_shards[layer], GROUP, axis=0, tiled=True)  257 us
    dot_general x4, matrix products, layer_backward(): jnp.einsum('th,fh->tf', d_resid, full_down, preferred_element_type=jnp.fl...  45.5 us
    dot_general x4, matrix products, layer_forward(): jnp.dot(low_rank, adapt_b, precision=FULL_PRECISION, preferred_element_ty...  39.1 us
    dot_general x4, matrix products, layer_forward(): jnp.dot(hidden_act, full_down, preferred_element_type=jnp.float32)  37.4 us
    dot_general x4, matrix products, layer_backward(): jnp.einsum('tf,hf->th', d_pre, full_up, preferred_element_type=jnp.float32)  37.2 us
    dot_general x4, matrix products, layer_forward(): jnp.dot(normed, full_up, preferred_element_type=jnp.float32)  29.1 us
  transfers between devices with their start and end apart: 18, of which 11 were waited for; matrix products, arithmetic and copies ran while one was open for 24% of the time, Pallas kernels for 0%

commit v1 on v0

v1 whole, which is shorter than its diff:
```python
import jax
import jax.numpy as jnp
from jax import lax
from jax.experimental import pallas as pl
from jax.experimental.pallas import tpu as pltpu
from jax.sharding import PartitionSpec as P

GROUP = ("data", "local")
EPS = 1e-6
MESH_ID = pl.DeviceIdType.MESH
F32 = jnp.float32
BF16 = jnp.bfloat16
H = 1024
FH = 2048
NT = 1024
GT = 256
LAYERS = RING = 4
CR = 256
UNIT = 512
LANE = 128
SUB = 8
RB = 128
QW = 768
GROUPS = ((0, 2), (2, 2))
COLS_UP = ((0, 640), (640, 640), (1280, 768))
COLS_DOWN = ((0, 384), (384, 384), (768, 256))
GELU_K = 0.7978845608028654
GELU_C = 0.044715


def split3(val):
    hi = val.astype(BF16).astype(F32)
    rest = val - hi
    mid = rest.astype(BF16).astype(F32)
    return hi, mid, (rest - mid).astype(BF16).astype(F32)


def gelu(pre):
    sq = pre * pre
    t = jnp.tanh(pre * (GELU_K + (GELU_K * GELU_C) * sq))
    return pre * (0.5 * t + 0.5)


def gelu_grad(pre):
    sq = pre * pre
    t = jnp.tanh(pre * (GELU_K + (GELU_K * GELU_C) * sq))
    slope = 0.5 * GELU_K + (1.5 * GELU_K * GELU_C) * sq
    return (0.5 * t + 0.5) + pre * ((1.0 - t * t) * slope)


def lane_sum3(rep):
    return rep + pltpu.roll(rep, 120, 1) + pltpu.roll(rep, 112, 1)


def spread(val):
    hi, mid, lo = split3(val)
    lane = lax.broadcasted_iota(jnp.int32, val.shape, 1)
    out = jnp.where(lane < 24, hi, jnp.where(lane < 48, mid, jnp.where(lane < 72, lo, 0.0)))
    return out.astype(BF16)


def span(i, n):
    return pl.ds(pl.multiple_of(i * n, n), n)


def ring(c, delta):
    return lax.rem(c + delta, RING)


def parts_sum(g):
    return g[0:SUB] + g[24:32] + g[48:56]


def dot(a, b):
    return lax.dot_general(a, b, (((1,), (0,)), ((), ())), preferred_element_type=F32)


def dot_nt(a, b):
    return lax.dot_general(a, b, (((1,), (1,)), ((), ())), preferred_element_type=F32)


def dot_tn(a, b):
    return lax.dot_general(a, b, (((0,), (0,)), ((), ())), preferred_element_type=F32)


def kernel(tok, cot, up, down, arep, bhalf,
           out, gout, grads, presave,
           w1, w2, apat, bpat, stage_a, stage_b, ubuf, dbuf, sbuf, pre, ybuf, yrecv, dl, dlrecv, vbuf, xbuf,
           gpart, rz, ry, rx, rsum, rpart,
           lsem, xsem, gssem, grsem, ysend, yrecv_sem, usend, urecv, dsend, drecv, lsend, lrecv, psem, osem, assem, arsem, prsem):
    d = lax.axis_index("data")
    j = lax.axis_index("local")
    oth = 1 - j
    y = d // RING
    z, y, x = y // RING, ring(y, 0), ring(d, 0)
    me = (z, y, x)

    def data_id(dim, delta):
        c = list(me)
        c[dim] = ring(c[dim], delta + RING)
        return {"data": (c[0] * RING + c[1]) * RING + c[2]}

    partner = {"local": oth}

    def remote(src, dst, ss, rs, dev):
        return pltpu.make_async_remote_copy(src_ref=src, dst_ref=dst, send_sem=ss, recv_sem=rs, device_id=dev, device_id_type=MESH_ID)

    def block(p, k, v, l0, nl, mat):
        dims = [None] * 3
        for i in range(3):
            q = (p + i) % 3
            dims[q] = slice(None) if i < k else (v if i == k else me[q])
        c0, cn = (COLS_UP if mat == 0 else COLS_DOWN)[p]
        return (w1, w2)[mat].at[pl.ds(l0, nl), dims[0], dims[1], dims[2], :, pl.ds(c0, cn)]

    def hop(p, k, v, g, l0, nl, mat, msg, delta):
        r = block(p, k, v, l0, nl, mat)
        return remote(r, r, gssem.at[mat, k], grsem.at[p, k, msg, g], data_id((p + k) % 3, delta))

    def full(k, g, l0, nl):
        for p in range(3):
            c = me[(p + k) % 3]
            hop(p, k, c, g, l0, nl, 0, 0, 1).start()
            hop(p, k, c, g, l0, nl, 1, 3, -1).start()
            hop(p, k, c, g, l0, nl, 0, 1, -1).start()
            hop(p, k, c, g, l0, nl, 1, 2, 1).start()

    def forward_half(k, g, l0, nl):
        for p in range(3):
            c = me[(p + k) % 3]
            left, right = ring(c, 3), ring(c, 1)
            hop(p, k, left, g, l0, nl, 0, 0, 1).wait_recv()
            hop(p, k, left, g, l0, nl, 0, 4, 1).start()
            hop(p, k, right, g, l0, nl, 1, 3, -1).wait_recv()
            hop(p, k, right, g, l0, nl, 1, 5, -1).start()

    def arrive(k, g, l0, nl):
        for p in range(3):
            c = me[(p + k) % 3]
            left, right, opp = ring(c, 3), ring(c, 1), ring(c, 2)
            hop(p, k, right, g, l0, nl, 0, 1, -1).wait_recv()
            hop(p, k, left, g, l0, nl, 1, 2, 1).wait_recv()
            hop(p, k, opp, g, l0, nl, 0, 4, 1).wait_recv()
            hop(p, k, opp, g, l0, nl, 1, 5, -1).wait_recv()

    def drain_gather():
        for mat, ref in ((0, w1), (1, w2)):
            for k, r in ((0, ref.at[:, 0, 0, 0:3]), (1, ref.at[:, 0, 0:3]), (2, ref.at[:, 0:3])):
                remote(r, r, gssem.at[mat, k], grsem.at[0, 0, 0, 0], data_id(0, 1)).wait_send()

    loads = [
        pltpu.make_async_copy(up.at[j], w1.at[:, z, y, x, span(j, SUB)], lsem.at[0]),
        pltpu.make_async_copy(down, w2.at[:, z, y, x], lsem.at[1]),
        pltpu.make_async_copy(tok, xbuf.at[0], lsem.at[2]),
        pltpu.make_async_copy(cot, dbuf.at[:, j], lsem.at[3]),
        pltpu.make_async_copy(arep, stage_a, lsem.at[4]),
        pltpu.make_async_copy(bhalf.at[j], stage_b, lsem.at[5]),
    ]
    for c in loads:
        c.start()
    bar = pltpu.get_barrier_semaphore()
    for dim in range(3):
        for delta in (1, 2, 3):
            pl.semaphore_signal(bar, inc=1, device_id=data_id(dim, delta), device_id_type=MESH_ID)
    pl.semaphore_signal(bar, inc=1, device_id=partner, device_id_type=MESH_ID)
    pl.semaphore_wait(bar, 10)

    mine_rows = w1.at[:, z, y, x, span(j, SUB)]
    other_rows = w1.at[:, z, y, x, span(oth, SUB)]
    ex_up = remote(up.at[oth], mine_rows, xsem.at[0], xsem.at[1], partner)
    ex_up.start()
    loads[0].wait()
    loads[1].wait()
    remote(up.at[oth], other_rows, xsem.at[0], xsem.at[1], partner).wait_recv()
    for g, (l0, nl) in enumerate(GROUPS):
        full(0, g, l0, nl)
    ex_cot = remote(cot, dbuf.at[:, j], xsem.at[2], xsem.at[3], partner)
    ex_cot.start()

    def inv_rms(xf):
        return lax.rsqrt(jnp.mean(xf * xf, axis=-1, keepdims=True) + EPS)

    def u_copy(c):
        return remote(ubuf.at[c, j], ubuf.at[c, j], usend.at[c], urecv.at[c], partner)

    def u_arrival(c):
        return remote(ubuf.at[c, oth], ubuf.at[c, oth], usend.at[c], urecv.at[c], partner)

    def y_copy(c):
        return remote(ybuf.at[oth], yrecv.at[c], ysend.at[0], yrecv_sem.at[c], partner)

    def l_copy(c):
        return remote(dl.at[oth], dlrecv.at[c], lsend.at[0], lrecv.at[c], partner)

    def d_copy(c):
        return remote(dbuf.at[c, j], dbuf.at[c, j], dsend.at[c], drecv.at[c], partner)

    def d_arrival(c):
        return remote(dbuf.at[c, oth], dbuf.at[c, oth], dsend.at[c], drecv.at[c], partner)

    def out_copy(c):
        return pltpu.make_async_copy(ubuf.at[c, j], out.at[c], osem.at[c])

    def gout_copy(c):
        return pltpu.make_async_copy(dbuf.at[c, j], gout.at[c], osem.at[2 + c])

    def send_u(l, c):
        @pl.loop(0, CR // RB)
        def _(i):
            rows = span(i, RB)
            xf = xbuf[l, c, rows].astype(F32)
            ubuf[c, j, rows] = (xf * inv_rms(xf)).astype(BF16)
        u_copy(c).start()

    loads[2].wait()
    for c in (0, 1):
        send_u(0, c)
    for g, (l0, nl) in enumerate(GROUPS):
        forward_half(0, g, l0, nl)

    loads[4].wait()
    loads[5].wait()

    @pl.loop(0, LAYERS * SUB)
    def _(i):
        l, r = i // SUB, span(lax.rem(i, SUB), LANE)
        hi, mid, lo = split3(stage_a[l, r])
        group = lax.rem(lax.broadcasted_iota(jnp.int32, (LANE, LANE), 1) // SUB, 3)
        apat[l, r] = jnp.where(group == 0, hi, jnp.where(group == 1, mid, lo)).astype(BF16)

    @pl.loop(0, LAYERS * SUB)
    def _(i):
        l, r = i // SUB, span(lax.rem(i, SUB), CR)
        parts = split3(stage_b[l, :, r])
        bpat[l, :, r] = jnp.concatenate([parts[m % 3] for m in range(16)], axis=0).astype(BF16)

    for g, (l0, nl) in enumerate(GROUPS):
        arrive(0, g, l0, nl)
        full(1, g, l0, nl)
    for g, (l0, nl) in enumerate(GROUPS):
        forward_half(1, g, l0, nl)
    arrive(1, 0, 0, 2)
    full(2, 0, 0, 1)
    full(2, 1, 1, 1)
    arrive(1, 1, 2, 2)
    forward_half(2, 0, 0, 1)
    full(2, 2, 2, 1)

    def ncol(n):
        return span(n, NT)

    def w1_tile(l, n):
        return w1[l, :, :, :, :, ncol(n)].reshape(H, NT)

    def w2_tile(l, n):
        return w2[l, :, :, :, :, ncol(n)].reshape(FH, NT)

    def pre_save(l, c):
        return pltpu.make_async_copy(pre.at[c], presave.at[l, c], psem.at[c])

    def pre_load(l, c):
        return pltpu.make_async_copy(presave.at[l, c], pre.at[c], psem.at[c])

    def up_phase(l, c):
        u = ubuf[c].reshape(UNIT, H)
        vsplit = spread(lane_sum3(dot(u, apat[l])))
        vbuf[l, c] = vsplit

        @pl.when(l > 0)
        def _():
            pre_save(l - 1, c).wait()

        @pl.loop(0, FH // NT)
        def _(n):
            acc = dot(ubuf[c].reshape(UNIT, H), w1_tile(l, n)) + dot(vbuf[l, c], bpat[l, :, ncol(n)])
            a = acc.astype(BF16)
            pre[c, :, ncol(n)] = a
            sbuf[:, ncol(n)] = gelu(a.astype(F32)).astype(BF16)

        @pl.when(l < LAYERS - 1)
        def _():
            pre_save(l, c).start()

    def down_phase(l, c):
        @pl.loop(0, H // NT)
        def _(n):
            ybuf[:, :, ncol(n)] = dot(sbuf[...], w2_tile(l, n)).reshape(2, CR, NT)
        y_copy(c).start()

    def finish(l, c):
        y_copy(c).wait_recv()
        u_copy(c).wait_send()

        @pl.loop(0, CR // RB)
        def _(i):
            rows = span(i, RB)
            new = (xbuf[l, c, rows].astype(F32) + (ybuf[j, rows] + yrecv[c, rows])).astype(BF16)

            @pl.when(l < LAYERS - 1)
            def _():
                xbuf[l + 1, c, rows] = new
                xf = new.astype(F32)
                ubuf[c, j, rows] = (xf * inv_rms(xf)).astype(BF16)

            @pl.when(l == LAYERS - 1)
            def _():
                ubuf[c, j, rows] = new

        @pl.when(l < LAYERS - 1)
        def _():
            u_copy(c).start()

        @pl.when(l == LAYERS - 1)
        def _():
            out_copy(c).start()

    @pl.loop(0, LAYERS)
    def _(l):
        @pl.when(l + 1 < LAYERS)
        def _():
            forward_half(2, l + 1, l + 1, 1)

        @pl.when(l + 3 < LAYERS)
        def _():
            full(2, l + 3, l + 3, 1)

        arrive(2, l, l, 1)
        u_arrival(0).wait_recv()
        up_phase(l, 0)

        @pl.when(l > 0)
        def _():
            finish(l - 1, 1)
            y_copy(1).wait_send()

        down_phase(l, 0)
        u_arrival(1).wait_recv()
        up_phase(l, 1)
        finish(l, 0)
        y_copy(0).wait_send()
        down_phase(l, 1)

    def dpre_phase(l, c):
        @pl.when(l < LAYERS - 1)
        def _():
            pre_load(l, c).wait()

        @pl.loop(0, FH // NT)
        def _(n):
            w = w2[l, span(n, NT // UNIT)].reshape(NT, H)
            dh = dot_nt(dbuf[c].reshape(UNIT, H), w).astype(BF16).astype(F32)
            a = pre[c, :, ncol(n)].astype(F32)
            sbuf[:, ncol(n)] = (gelu_grad(a) * dh).astype(BF16)

        @pl.when(l > 0)
        def _():
            pre_load(l - 1, c).start()

    def low_phase(l, c):
        dl[...] = lane_sum3(dot_nt(sbuf[...], bpat[l])).reshape(2, CR, LANE)
        l_copy(c).start()
        for t in range(FH // GT):
            g = parts_sum(dot_tn(vbuf[l, c], sbuf[:, pl.ds(t * GT, GT)]))
            dst = (l, t // 3, slice(None), pl.ds((t % 3) * GT, GT))
            gpart[dst] = gpart[dst] + g if c else g

    def dmain_phase(l, c):
        @pl.loop(0, H // NT)
        def _(n):
            w = w1[l, span(n, NT // CR)].reshape(NT, FH)
            ybuf[:, :, ncol(n)] = dot_nt(sbuf[...], w).reshape(2, CR, NT)
        y_copy(c).start()

    def back_finish(l, c):
        l_copy(c).wait_recv()
        y_copy(c).wait_recv()
        dlow = dl[j] + dlrecv[c]
        dsplit = spread(dlow)

        @pl.when(l < LAYERS - 1)
        def _():
            d_copy(c).wait_send()

        @pl.when(l == LAYERS - 1)
        def _():
            out_copy(c).wait()

        @pl.loop(0, CR // RB)
        def _(i):
            rows = span(i, RB)
            xf = xbuf[l, c, rows].astype(F32)
            inv = inv_rms(xf)
            ubuf[c, j, rows] = (xf * inv).astype(BF16)
            dl[j, rows] = dl[j, rows] + dlrecv[c, rows]
            dside = dot_nt(spread(dl[j, rows]), apat[l]).astype(BF16).astype(F32)
            dmain = (ybuf[j, rows] + yrecv[c, rows]).astype(BF16).astype(F32)
            dn = (dmain + dside).astype(BF16).astype(F32)
            rowdot = jnp.mean(xf * dn, axis=-1, keepdims=True)
            dx = dbuf[c, j, rows].astype(F32) + inv * dn - xf * (inv * inv * inv) * rowdot
            dbuf[c, j, rows] = dx.astype(BF16)

        @pl.when(l > 0)
        def _():
            d_copy(c).start()

        @pl.when(l == 0)
        def _():
            gout_copy(c).start()

        for t in range(H // GT):
            g = parts_sum(dot_tn(dsplit, ubuf[c, j, :, pl.ds(t * GT, GT)]))
            tt = t + FH // GT
            dst = (l, tt // 3, slice(None), pl.ds((tt % 3) * GT, GT))
            gpart[dst] = gpart[dst] + g if c else g

    def line_copies(l, stage, dim, src, dst_buf):
        return [remote(src(ring(me[dim], k)), dst_buf.at[l, me[dim]], assem.at[stage, l, k - 1], arsem.at[stage, l, k - 1], data_id(dim, k)) for k in (1, 2, 3)]

    def line_wait(l, stage, dim, buf):
        for k in (1, 2, 3):
            v = ring(me[dim], RING - k)
            remote(buf.at[l, v], buf.at[l, v], assem.at[stage, l, k - 1], arsem.at[stage, l, k - 1], data_id(dim, k)).wait_recv()

    def sum4(buf, l):
        return (buf[l, 0] + buf[l, 1]) + (buf[l, 2] + buf[l, 3])

    def reduce_stage(l, s):
        if s == 0:
            for cp in line_copies(l, 0, 0, lambda q: gpart.at[l, q], rz):
                cp.start()
            rz[l, z] = gpart[l, z]
        elif s == 1:
            line_wait(l, 0, 0, rz)
            ry[l, y] = sum4(rz, l)
            for cp in line_copies(l, 1, 1, lambda q: ry.at[l, y], ry):
                cp.start()
        elif s == 2:
            line_wait(l, 1, 1, ry)
            rx[l, x] = sum4(ry, l)
            for cp in line_copies(l, 2, 2, lambda q: rx.at[l, x], rx):
                cp.start()
        elif s == 3:
            line_wait(l, 2, 2, rx)
            rsum[l, z] = sum4(rx, l)
            for cp in line_copies(l, 3, 0, lambda q: rsum.at[l, z], rsum):
                cp.start()
        elif s == 4:
            line_wait(l, 3, 0, rsum)
            remote(rsum.at[l], rpart.at[l], prsem.at[0, l], prsem.at[1, l], partner).start()
            pltpu.make_async_copy(rsum.at[l], grads.at[j, l], prsem.at[2, l]).start()
        else:
            remote(rsum.at[l], rpart.at[l], prsem.at[0, l], prsem.at[1, l], partner).wait_recv()
            pltpu.make_async_copy(rpart.at[l], grads.at[oth, l], prsem.at[3, l]).start()

    ex_cot_in = remote(cot, dbuf.at[:, oth], xsem.at[2], xsem.at[3], partner)
    loads[3].wait()
    ex_cot_in.wait_recv()
    ex_cot.wait_send()
    ex_up.wait_send()

    def back_layer(l, last):
        not_top = l < LAYERS - 1

        @pl.when(not_top)
        def _():
            d_arrival(0).wait_recv()

        dpre_phase(l, 0)

        @pl.when(l == LAYERS - 1)
        def _():
            finish(LAYERS - 1, 1)

        @pl.when(not_top)
        def _():
            back_finish(l + 1, 1)
            l_copy(1).wait_send()
            reduce_stage(l + 1, 0)

        y_copy(1).wait_send()
        low_phase(l, 0)
        dmain_phase(l, 0)

        @pl.when(not_top)
        def _():
            reduce_stage(l + 1, 1)
            d_arrival(1).wait_recv()

        dpre_phase(l, 1)

        @pl.when(not_top)
        def _():
            reduce_stage(l + 1, 2)

        back_finish(l, 0)
        l_copy(0).wait_send()
        y_copy(0).wait_send()
        low_phase(l, 1)

        @pl.when(not_top)
        def _():
            reduce_stage(l + 1, 3)

        dmain_phase(l, 1)

        @pl.when(not_top)
        def _():
            reduce_stage(l + 1, 4)
            reduce_stage(l + 1, 5)

    @pl.loop(0, LAYERS)
    def _(i):
        back_layer(LAYERS - 1 - i, False)

    back_finish(0, 1)
    for s in range(6):
        reduce_stage(0, s)
    l_copy(1).wait_send()
    y_copy(1).wait_send()
    for c in (0, 1):
        gout_copy(c).wait()

    @pl.loop(0, LAYERS)
    def _(l):
        for s in range(4):
            for k in range(3):
                r = rz.at[l, 0]
                remote(r, r, assem.at[s, l, k], arsem.at[s, l, k], data_id(0, 1)).wait_send()
        remote(rsum.at[l], rpart.at[l], prsem.at[0, l], prsem.at[1, l], partner).wait_send()
        pltpu.make_async_copy(rsum.at[l], grads.at[j, l], prsem.at[2, l]).wait()
        pltpu.make_async_copy(rpart.at[l], grads.at[oth, l], prsem.at[3, l]).wait()

    drain_gather()


TWO = (2,)
PERM = (3, 0, 1, 2, 4)


def device_step(tokens, cotangent, up_shards, down_shards, lora_a, lora_b):
    up = jnp.transpose(up_shards.reshape(LAYERS, SUB, 64, 2, 32), PERM).reshape(2, LAYERS, SUB, FH)
    bhalf = jnp.transpose(lora_b.reshape(LAYERS, SUB, 64, 2, 32), PERM).reshape(2, LAYERS, SUB, FH)
    arep = jnp.tile(lora_a, (1, 1, 16))
    hbm = pl.BlockSpec(memory_space=pl.ANY)
    dma = pltpu.SemaphoreType.DMA
    out, gout, grads, _ = pl.pallas_call(
        kernel,
        out_shape=(
            jax.ShapeDtypeStruct((2, CR, H), BF16),
            jax.ShapeDtypeStruct((2, CR, H), BF16),
            jax.ShapeDtypeStruct((2, LAYERS, 4, SUB, QW), F32),
            jax.ShapeDtypeStruct((LAYERS - 1, 2, UNIT, FH), BF16),
        ),
        in_specs=[hbm] * 6,
        out_specs=[hbm] * 4,
        scratch_shapes=[
            pltpu.VMEM((LAYERS, RING, RING, RING, 16, FH), BF16),
            pltpu.VMEM((LAYERS, RING, RING, RING, 32, H), BF16),
            pltpu.VMEM((LAYERS, H, LANE), BF16),
            pltpu.VMEM((LAYERS, LANE, FH), BF16),
            pltpu.VMEM((LAYERS, H, LANE), F32),
            pltpu.VMEM((LAYERS, SUB, FH), F32),
            pltpu.VMEM((2, 2, CR, H), BF16),
            pltpu.VMEM((2, 2, CR, H), BF16),
            pltpu.VMEM((UNIT, FH), BF16),
            pltpu.VMEM((2, UNIT, FH), BF16),
            pltpu.VMEM((2, CR, H), F32),
            pltpu.VMEM((2, CR, H), F32),
            pltpu.VMEM((2, CR, LANE), F32),
            pltpu.VMEM((2, CR, LANE), F32),
            pltpu.VMEM((LAYERS, 2, UNIT, LANE), BF16),
            pltpu.VMEM((LAYERS, 2, CR, H), BF16),
        ] + [pltpu.VMEM((LAYERS, 4, SUB, QW), F32)] * 6 + [
            dma((6,)), dma((LAYERS,)), dma((2, 3)), dma((3, 3, 6, LAYERS)),
            dma((1,)), dma(TWO), dma(TWO), dma(TWO), dma(TWO), dma(TWO), dma((1,)), dma(TWO),
            dma(TWO), dma((LAYERS,)), dma((LAYERS, LAYERS, 3)), dma((LAYERS, LAYERS, 3)), dma((LAYERS, LAYERS)),
        ],
        compiler_params=pltpu.CompilerParams(collective_id=0, has_side_effects=True, vmem_limit_bytes=67000000),
    )(tokens.reshape(2, CR, H), cotangent.reshape(2, CR, H), up, down_shards, arep, bhalf)
    g = jnp.transpose(grads, (0, 1, 3, 2, 4)).reshape(2, LAYERS, 8, 3072)
    grad_b = jnp.transpose(g[..., :FH].reshape(2, LAYERS, 8, 64, 32), (1, 2, 3, 0, 4)).reshape(LAYERS, 8, 4096)
    grad_a = jnp.transpose(g[0, :, :, FH:] + g[1, :, :, FH:], (0, 2, 1))
    return out.reshape(UNIT, H), gout.reshape(UNIT, H), grad_a, grad_b


def solution(mesh):
    tok_spec = P(GROUP, None)
    weight_spec = P(None, GROUP, None)
    return jax.shard_map(device_step, mesh=mesh, in_specs=(tok_spec, tok_spec, weight_spec, weight_spec, P(), P()),
                         out_specs=(tok_spec, tok_spec, P(), P()), check_vma=False)
```

time: 1120 us -> 296 us (0.26)
  waiting for transfers between devices: 810 us -> 0 us
  Pallas kernels: 0 us -> 269 us
  matrix products: 237 us -> 0 us
  local copies, waits for them, and re-layouts: 43.2 us -> 24.5 us
  between operations: 15 us -> 0.71 us
    all_gather x16 -> x0, waiting for transfers between devices: 518 us -> none  [the longest x4 259 us: device_step(): full_up = lax.all_gather(up_shards[layer], GROUP, axis=0, tiled=True)]
    psum x2 -> x0, waiting for transfers between devices: 287 us -> none  [device_step(): grad_a, grad_b = lax.psum((grad_a, grad_b), GROUP)]
    pallas_call x0 -> x1, Pallas kernels: none -> 269 us  [device_step(): pl.pallas_call(kernel, out_shape=(jax.ShapeDtypeStruct((2, CR, H), BF16),...]
    dot_general x40 -> x0, matrix products: 237 us -> none  [the longest x4 45.5 us: layer_backward(): jnp.einsum('th,fh->tf', d_resid, full_down, preferred_element_type=jnp.fl...]
    dynamic_slice x8 -> x0, local copies, waits for them, and re-layouts: 33.1 us -> none  [the longest x4 16.7 us: device_step(): lax.dynamic_slice_in_dim(full_up, local_idx * up_rows, up_rows, axis=0)]
    reshape x0 -> x6, local copies, waits for them, and re-layouts: none -> 14.3 us  [the longest x1 5.18 us: device_step(): jnp.transpose(g[..., :FH].reshape(2, LAYERS, 8, 64, 32), (1, 2, 3, 0, 4))]
  transfers between devices with their start and end apart: 18 -> 0, of which waited for: 11 -> 0; matrix products, arithmetic and copies ran while one was open for 24% -> 0% of each run, Pallas kernels for 0% -> 0%
where the time goes in v1:
time: 296 us
  Pallas kernels  269 us (91%)
  local copies, waits for them, and re-layouts  24.5 us (8%)
    pallas_call x1, Pallas kernels, device_step(): pl.pallas_call(kernel, out_shape=(jax.ShapeDtypeStruct((2, CR, H), BF16),...  269 us

profile of v1, /device:TPU:1, one launch (start us, length us, event | category | flops | bytes accessed | tf_op | source)
XLA Modules:
  0.0 295.7 jit_solution(5768810489696750730)
XLA Ops:
  0.6 0.0 copy-start.3
  0.6 1.7 reshape.48
  2.4 0.3 copy.14
  2.7 1.8 reshape.49.up
  4.5 0.0 copy-done.3
  4.5 0.2 broadcast_bitcast_fusion
  4.7 0.0 copy-start.2
  4.8 1.8 copy.16.arep
  6.6 0.0 copy-done.2
  6.6 3.1 %reshape.50 = f32[4,8,64,2,32]{4,3,2,1,0:T(2,128)} reshape(f32[4,8,4096]{2,1,0:T(8,128)S(1)} %copy-done.2) | data formatting | bytes 1048576 | tf_op jit(solution)/shard_map/reshape | solution.py:542
  9.7 1.9 copy.15
  11.6 1.8 reshape.51.bhalf
  13.3 268.9 %shard_map.93 = (bf16[2,256,1024]{2,1,0:T(8,128)(2,1)}, bf16[2,256,1024]{2,1,0:T(8,128)(2,1)}, f32[2,4,4,8,768]{4,3,2,1,0:T(8,128)}, bf16[3,2,512,2048]{3,2,1,0:T(8,128)(2,1)}) custom-call(bf16[2,256,1024]{2,1,0:T(8,128)(2,1)} %bitcast.25, bf16[2,256,1024]{2,1,0:T(8,128)(2,1)} %bitcast.26, bf16[2,4,8,2048]{3,2,1,0:T(8,128)(2,1)} %reshape.49.up, ...), custom_call_target="tpu_custom_call" | custom-call | tf_op jit(solution)/shard_map/pallas_call | solution.py:546
  282.2 1.6 fusion
  283.9 1.1 slice.14
  284.9 0.7 reshape.55
  285.6 3.0 %copy.17 = f32[4,8,64,2,32]{4,3,2,1,0:T(2,128)} copy(f32[4,8,64,2,32]{4,2,1,0,3:T(8,128)S(1)} %bitcast.22) | data formatting | bytes 1048576 | tf_op jit(solution)/shard_map/transpose | solution.py:581
  288.6 0.0 copy-start.1
  288.6 0.0 copy-start
  288.6 5.2 %reshape.56 = f32[4,8,4096]{2,1,0:T(8,128)} reshape(f32[4,8,64,2,32]{4,3,2,1,0:T(2,128)} %copy.17) | data formatting | bytes 1048576 | tf_op jit(solution)/shard_map/reshape | solution.py:581
  293.8 0.0 copy-done.1
  293.8 1.0 copy.20
  294.8 0.0 copy-done
  294.8 1.0 copy.21
Async XLA Ops:
  0.6 3.9 %copy-start.3 = (f32[4,1024,8]{1,2,0:T(8,128)S(1)}, f32[4,1024,8]{1,2,0:T(8,128)}, u32[]{:S(2)}) copy-start(f32[4,1024,8]{1,2,0:T(8,128)} %param.10) | copy-start | bytes 393220
  4.7 1.9 copy-start.2
  288.6 5.2 %copy-start.1 = (bf16[2,256,1024]{2,1,0:T(8,128)(2,1)S(1)}, bf16[2,256,1024]{2,1,0:T(8,128)(2,1)}, u32[]{:S(2)}) copy-start(bf16[2,256,1024]{2,1,0:T(8,128)(2,1)} %get-tuple-element.7) | copy-start | bytes 3145732
  288.6 6.2 %copy-start = (bf16[2,256,1024]{2,1,0:T(8,128)(2,1)S(1)}, bf16[2,256,1024]{2,1,0:T(8,128)(2,1)}, u32[]{:S(2)}) copy-start(bf16[2,256,1024]{2,1,0:T(8,128)(2,1)} %get-tuple-element.8) | copy-start | bytes 3145732
